TPU v7x, 256 devices: a whole 4x4x8 slice. The times are simulated.
256 devices in a mesh: node: 32 (over z, x_lo, core), expert: 8 (over x_hi, y).
Axes of the slice: x: 4 (x_hi: 2, x_lo: 2; x = x_hi * 2 + x_lo), y: 4, z: 8, core: 2. Of those that a mesh axis runs over, the one named last changes fastest.
Arguments:
- numerators: bfloat16 [32, 8, 1536, 1536], P('node', 'expert'), may hold values from -6 to 6
- push_weights: float32 [32], replicated, may hold values from 0.5 to 2
- tokens: bfloat16 [32, 1024, 1536], P('node', 'expert'), may hold values from -6 to 6
- cotangent: bfloat16 [32, 1024, 1536], P('node', 'expert'), may hold values from -6 to 6
- routing: int32 [32, 1024, 2], P('node', 'expert'), may hold values from 0 to 7, all different within a row; in each aligned block of 128 rows (0 to 127, 128 to 255, ..., all dimensions but the last counted through in order) at most 41 rows name the same one
- gates: float32 [32, 1024, 2], P('node', 'expert'), may hold values from 0.1 to 1
Outputs:
- averaged: float32 [8, 1536, 1536], P('expert', 'node')
Inputs may be any that keep to these rules, and one draw needn't show every extreme that they name: `routing`: each row names 2 different experts; in each aligned block of 128 rows (the rows of one device) no expert is named by more than 41 rows, and in some block some expert is named by exactly 41 rows.
All inputs are finite; a program needn't handle non-finite values.
Results may differ from a plain program's by a relative error of at most 0.007.
The roundings to bfloat16 on the way count: a program that leaves them out, or rounds other values in their place, can miss the bound.
Values may be sent and summed in bfloat16 or wider, within the bound.
A program may use at most 64 MiB of HBM per device.

v0:
```python
import math

import jax
import jax.numpy as jnp
from jax import lax
from jax.sharding import PartitionSpec as P

ROUNDS = 2


step_size = 1.0


def side_by_side(arrays, axis, split_dim, concat_dim, along):
    both = jnp.concatenate(arrays, axis=along)
    out, at, done = (
        lax.all_to_all(both, axis, split_axis=split_dim, concat_axis=concat_dim, tiled=True),
        0,
        [],
    )
    for a in arrays:
        done.append(lax.slice_in_dim(out, at, at + a.shape[along], axis=along))
        at += a.shape[along]
    return tuple(done)


def passed_along(shard, axis, by):
    count = lax.axis_size(axis)
    return lax.ppermute(shard, axis, [(i, (i + by) % count) for i in range(count)])


def in_blocks(shard, dim, count):
    before, after = (shard.shape[:dim], shard.shape[dim + 1 :])
    return jnp.moveaxis(shard.reshape(*before, count, -1, *after), dim, 0)


def sent_and_summed(shard, axis, dim):
    parts = in_blocks(shard, dim, lax.axis_size(axis))
    arrived = lax.all_to_all(parts, axis, split_axis=0, concat_axis=0, tiled=True)
    return arrived.astype(jnp.float32).sum(axis=0)


def expert_grads(weights, buffer_inputs, buffer_gradients):
    hidden_units = weights.shape[2] // 3
    model_scale = 1.0 / math.sqrt(weights.shape[1])
    hidden_scale = 1.0 / math.sqrt(hidden_units)
    gate_weight_matrix = weights[:, :, :hidden_units]
    upward_weight = weights[:, :, hidden_units : 2 * hidden_units]
    downward_weight = weights[:, :, 2 * hidden_units :]
    gate_pre = (
        jnp.einsum(
            "wqv,qvy->wqy", buffer_inputs, gate_weight_matrix, preferred_element_type=jnp.float32
        )
        * model_scale
    )
    upper_pre = (
        jnp.einsum("wqv,qvy->wqy", buffer_inputs, upward_weight, preferred_element_type=jnp.float32)
        * model_scale
    )
    sigmoid_gate = jax.nn.sigmoid(gate_pre)
    gated_hidden = (gate_pre * sigmoid_gate * upper_pre).astype(jnp.bfloat16)
    grad_down = (
        jnp.einsum(
            "jaw,jai->awi", buffer_gradients, gated_hidden, preferred_element_type=jnp.float32
        )
        * hidden_scale
    )
    grad_act = (
        jnp.einsum(
            "wqv,qvy->wqy", buffer_gradients, downward_weight, preferred_element_type=jnp.float32
        )
        * hidden_scale
    )
    gate_gradient = (
        grad_act * upper_pre * sigmoid_gate * (1.0 + gate_pre * (1.0 - sigmoid_gate))
    ).astype(jnp.bfloat16)
    upward_gradient = (grad_act * gate_pre * sigmoid_gate).astype(jnp.bfloat16)
    grad_wgate = (
        jnp.einsum("jaw,jai->awi", buffer_inputs, gate_gradient, preferred_element_type=jnp.float32)
        * model_scale
    )
    grad_wupper = (
        jnp.einsum(
            "jaw,jai->awi", buffer_inputs, upward_gradient, preferred_element_type=jnp.float32
        )
        * model_scale
    )
    return jnp.concatenate([grad_wgate, grad_wupper, grad_down], axis=2)


def local(numerators, push_weights, tokens, cotangent, routing, gates):
    node_count = lax.axis_size("node")
    node_index = lax.axis_index("node")
    local_experts = numerators.shape[1]
    expert_count = local_experts * lax.axis_size("expert")
    tok_rows = tokens.shape[1]
    choose = routing.shape[2]
    model_dim = tokens.shape[2]
    capacity = min(tok_rows, tok_rows * choose * 5 // (4 * expert_count) + 1)
    flat_routes = routing[0].reshape(-1)
    onehot = (flat_routes[:, None] == jnp.arange(expert_count, dtype=jnp.int32)[None, :]).astype(
        jnp.int32
    )
    ranking = jnp.sum((jnp.cumsum(onehot, axis=0) - 1) * onehot, axis=1)
    slot_ids = ranking * expert_count + flat_routes
    slot_table = (
        slot_ids[:, None] == jnp.arange(capacity * expert_count, dtype=jnp.int32)[None, :]
    ).astype(jnp.float32)
    slot_table = slot_table.reshape(tok_rows, choose, capacity * expert_count)
    placing = jnp.sum(slot_table, axis=1)
    slot_gate = jnp.sum(slot_table * gates[0][:, :, None], axis=(0, 1))
    joined = jnp.concatenate([tokens[0], cotangent[0]], axis=1)
    placed = jnp.dot(placing.T.astype(jnp.bfloat16), joined, preferred_element_type=jnp.float32)
    buffer_inputs = placed[:, :model_dim].astype(jnp.bfloat16)
    buffer_gradients = (placed[:, model_dim:] * slot_gate[:, None]).astype(jnp.bfloat16)
    buffer_inputs = buffer_inputs.reshape(capacity, expert_count, model_dim)
    buffer_gradients = buffer_gradients.reshape(capacity, expert_count, model_dim)
    recv_inputs, recv_grads = side_by_side((buffer_inputs, buffer_gradients), "expert", 1, 0, 2)
    current = numerators
    weights_now = push_weights
    pushed = numerators
    offset = 1
    mixed_weights = push_weights
    for round_index in range(ROUNDS):
        offset = 2**round_index
        own_weight = lax.dynamic_index_in_dim(weights_now, node_index, keepdims=False)
        params = (current.astype(jnp.float32) / own_weight).astype(jnp.bfloat16)
        gradients = expert_grads(params[0], recv_inputs, recv_grads)
        pushed = (current.astype(jnp.float32) - step_size * gradients[None]).astype(jnp.bfloat16)
        mixed_weights = (weights_now + jnp.roll(weights_now, offset)) / 2.0
        if round_index < ROUNDS - 1:
            arrived = passed_along(pushed, "node", offset)
            current = ((pushed.astype(jnp.float32) + arrived.astype(jnp.float32)) / 2.0).astype(
                jnp.bfloat16
            )
            weights_now = mixed_weights
    factor = (0.5 / mixed_weights + 0.5 / jnp.roll(mixed_weights, -offset)) / node_count
    own_factor = lax.dynamic_index_in_dim(factor, node_index, keepdims=False)
    summand = pushed.astype(jnp.float32) * own_factor
    return sent_and_summed(summand[0].astype(jnp.bfloat16), "node", 1)


def solution(mesh):
    placed = (
        P("node", "expert", None, None),
        P(),
        P("node", "expert", None),
        P("node", "expert", None),
        P("node", "expert", None),
        P("node", "expert", None),
    )
    return jax.shard_map(
        local, mesh=mesh, in_specs=placed, out_specs=P("expert", "node", None), check_vma=False
    )
```

profile of v0, /device:TPU:1, one launch (start us, length us, event | category | flops | bytes accessed | tf_op | source)
XLA Modules:
  0.0 250.1 jit_solution(2530537647644475692)
XLA Ops:
  0.0 0.8 copy.28
  1.1 0.6 reduce-window.6
  2.3 0.9 select_reduce_fusion
  3.1 1.8 fusion.33
  5.8 1.7 pad_maximum_fusion
  7.6 7.6 %all-to-all-start = ((bf16[41,8,3072]{2,0,1:T(8,128)(2,1)}), bf16[41,8,3072]{2,0,1:T(8,128)(2,1)S(1)}, u32[]{:S(2)}, u32[]{:S(2)}) async-start(bf16[41,8,3072]{2,0,1:T(8,128)(2,1)} %pad_maximum_fusion), calls=%async_computation | async-start | bytes 4718592 | tf_op jit(solution)/shard_map/all_to_all | solution.py:17
  15.2 0.7 fusion.56
  15.8 6.6 %copy.27 = bf16[1,1,1536,1536]{2,3,1,0:T(8,128)(2,1)} copy(bf16[1,1,1536,1536]{3,2,1,0:T(8,128)(2,1)} %param.6) | data formatting | bytes 9437184 | tf_op args[0]
  22.4 6.0 %fusion.5 = bf16[1,1536,1536]{1,2,0:T(8,128)(2,1)} fusion(bf16[1,1,1536,1536]{2,3,1,0:T(8,128)(2,1)} %copy.27, f32[]{:T(128)} %bitcast.11), kind=kLoop, calls=%fused_computation.14 | loop fusion | flops 7077888 | bytes 9437188 | tf_op jit(solution)/shard_map/squeeze | solution.py:128
  28.5 15.7 %all-to-all-done = bf16[41,8,3072]{2,0,1:T(8,128)(2,1)S(1)} async-done(((bf16[41,8,3072]{2,0,1:T(8,128)(2,1)}), bf16[41,8,3072]{2,0,1:T(8,128)(2,1)S(1)}, u32[]{:S(2)}, u32[]{:S(2)}) %all-to-all-start) | async-done | bytes 2015264 | tf_op jit(solution)/shard_map/all_to_all | solution.py:17
  44.2 1.9 all_to_all.19
  46.1 2.6 %fusion.24 = f32[328,1,512]{2,0,1:T(8,128)S(1)} fusion(bf16[1,1536,1536]{1,2,0:T(8,128)(2,1)} %fusion.5, bf16[328,1,3072]{2,0,1:T(8,128)(2,1)} %all_to_all.19), kind=kOutput, calls=%fused_computation.48 | convolution fusion | flops 516067328 | bytes 3252224 | tf_op jit(solution)/shard_map/wqv,qvy->wqy/dot_general | solution.py:51
  49.2 2.1 fusion.22
  51.3 0.7 fusion.20
  52.1 1.1 fusion.7
  53.2 1.2 fusion.6
  54.3 1.1 fusion.8
  55.4 1.8 fusion.1
  57.2 1.6 collective-permute-start
  58.9 0.7 fusion.46
  61.0 48.9 %collective-permute-done = bf16[1,1,1536,1536]{2,3,1,0:T(8,128)(2,1)S(1)} collective-permute-done((bf16[1,1,1536,1536]{2,3,1,0:T(8,128)(2,1)S(1)}, bf16[1,1,1536,1536]{2,3,1,0:T(8,128)(2,1)S(1)}, u32[]{:S(2)}, u32[]{:S(2)}) %collective-permute-start) | collective-permute-done | bytes 4718624 | tf_op jit(solution)/shard_map/ppermute | solution.py:29
  109.9 2.4 fusion.4
  112.3 0.7 fusion.30
  113.0 0.7 fusion.28
  113.8 0.7 fusion.26
  114.5 1.1 fusion.10
  115.6 1.2 fusion.9
  116.7 1.1 fusion.11
  117.8 4.5 %multiply_convert_fusion = bf16[1,1,1536,1536]{2,3,1,0:T(8,128)(2,1)} fusion(f32[1,1536,512]{1,2,0:T(8,128)S(1)} %fusion.11, f32[1,1536,512]{1,2,0:T(8,128)S(1)} %fusion.10, f32[1,1536,512]{1,2,0:T(8,128)S(1)} %fusion.9, f32[]{:T(128)} %bitcast.54, bf16[1,1,1536,1536]{2,3,1,0:T(8,128)(2,1)S(1)} %collective-permute-done, bf16[1,1,1536,1536]{2,3,1,0:T(8,128)(2,1)S(1)} %fusion.1), kind=kLoop, calls=%fused_computation.11 | loop fusion | flops 30670848 | bytes 23592964 | tf_op jit(solution)/shard_map/convert_element_type | solution.py:140
  122.3 6.7 %copy.34 = bf16[1,1,1536,1536]{3,2,1,0:T(8,128)(2,1)} copy(bf16[1,1,1536,1536]{2,3,1,0:T(8,128)(2,1)} %multiply_convert_fusion) | data formatting | bytes 9437184 | tf_op jit(solution)/shard_map/convert_element_type | solution.py:140
  129.0 119.7 %all_to_all.23 = bf16[32,1,48,1536]{3,2,1,0:T(8,128)(2,1)S(1)} all-to-all(bf16[32,1,48,1536]{3,2,1,0:T(8,128)(2,1)} %bitcast.159), channel_id=1, replica_groups=mesh['node'=32,'expert'=8] {'node'}, dimensions={0} | all-to-all | bytes 9437184 | tf_op jit(solution)/shard_map/all_to_all | solution.py:39
  248.7 1.4 convert_reduce_fusion
  (32 shorter events, 3.8 us)
Async XLA Ops:
  7.6 7.6 %copy-start.2 = (f32[32]{0:T(128)S(1)}, f32[32]{0:T(128)}, u32[]{:S(2)}) copy-start(f32[32]{0:T(128)} %param.7) | copy-start | bytes 388
  7.6 36.6 %all-to-all-start = ((bf16[41,8,3072]{2,0,1:T(8,128)(2,1)}), bf16[41,8,3072]{2,0,1:T(8,128)(2,1)S(1)}, u32[]{:S(2)}, u32[]{:S(2)}) async-start(bf16[41,8,3072]{2,0,1:T(8,128)(2,1)} %pad_maximum_fusion), calls=%async_computation | async-start | bytes 4718592 | tf_op jit(solution)/shard_map/all_to_all | solution.py:17
  46.1 3.1 %copy-start = (bf16[1,1536,1536]{1,2,0:T(8,128)(2,1)S(1)}, bf16[1,1536,1536]{1,2,0:T(8,128)(2,1)}, u32[]{:S(2)}) copy-start(bf16[1,1536,1536]{1,2,0:T(8,128)(2,1)} %fusion.5) | copy-start | bytes 14155780
  49.2 2.1 copy-start.1
  52.1 3.3 %slice-start = ((s8[4718592]{0:T(1024)(128)(4,1)}), s8[4194304]{0:T(1024)(128)(4,1)S(1)}, s32[]{:S(2)}) async-start(s8[4718592]{0:T(1024)(128)(4,1)} %bitcast.157), calls=%async_computation.2 | async-start | bytes 8388608
  53.1 2.3 slice-start.1
  57.2 52.7 %collective-permute-start = (bf16[1,1,1536,1536]{2,3,1,0:T(8,128)(2,1)S(1)}, bf16[1,1,1536,1536]{2,3,1,0:T(8,128)(2,1)S(1)}, u32[]{:S(2)}, u32[]{:S(2)}) collective-permute-start(bf16[1,1,1536,1536]{2,3,1,0:T(8,128)(2,1)S(1)} %fusion.1), channel_id=1, source_target_pairs={{0,8},{8,16},{16,24},{24,32},{32,40},{40,48},{48,56},{56,64},{64,7... | collective-permute-start | bytes 14155784 | tf_op jit(solution)/shard_map/ppermute | solution.py:29
where the time goes:
time: 251 us; the launch traced here: 250 us
  blocking collectives  120 us (48%)
  waiting for transfers between devices  64.6 us (26%)
  other arithmetic  20.4 us (8%)
  local copies, waits for them, and re-layouts  20 us (8%)
  matrix products  15.9 us (6%)
  starting transfers between devices  9.22 us (4%)
    all_to_all x1, blocking collectives, sent_and_summed(): lax.all_to_all(parts, axis, split_axis=0, concat_axis=0, tiled=True)  120 us
    ppermute x1, waiting for transfers between devices, passed_along(): lax.ppermute(shard, axis, [(i, (i + by) % count) for i in range(count)])  48.9 us
    all_to_all x1, waiting for transfers between devices, side_by_side(): lax.all_to_all(both, axis, split_axis=split_dim, concat_axis=concat_dim,...  15.7 us
    squeeze x2, other arithmetic, local(): gradients = expert_grads(params[0], recv_inputs, recv_grads)  8.42 us
    unnamed x12, local copies, waits for them, and re-layouts  7.97 us
    all_to_all x1, starting transfers between devices, side_by_side(): lax.all_to_all(both, axis, split_axis=split_dim, concat_axis=concat_dim,...  7.61 us
    convert_element_type x1, local copies, waits for them, and re-layouts, local(): return sent_and_summed(summand[0].astype(jnp.bfloat16), 'node', 1)  6.71 us
  transfers between devices with their start and end apart: 2, of which 2 were waited for; matrix products, arithmetic and copies ran while one was open for 6% of the time, Pallas kernels for 0%

commit v1 on v0

v1 whole, which is shorter than its diff:
```python
import functools
import math

import jax
import jax.numpy as jnp
from jax import lax
from jax.experimental import pallas as pl
from jax.experimental.pallas import tpu as pltpu
from jax.sharding import PartitionSpec as P

MESH = pl.DeviceIdType.MESH
LANES = 128
ROW_STEP = 384
F32 = jnp.float32
BF16 = jnp.bfloat16


def kernel(
    nodes,
    experts,
    slots,
    pw_ref,
    route_ref,
    gate_ref,
    tok_ref,
    cot_ref,
    num_ref,
    out_ref,
    x_out,
    g_out,
    x_in,
    g_in,
    x_tr,
    g_tr,
    zb,
    par,
    act,
    pushed,
    arrived,
    share,
    share_in,
    ring_out,
    ring_in,
    side_out,
    side_in,
    kept,
    load_sem,
    x_send,
    x_recv,
    g_send,
    g_recv,
    b_send,
    b_recv,
    c_send,
    c_recv,
    r_send,
    r_recv,
    s_send,
    s_recv,
):
    node = lax.axis_index("node")
    me = lax.axis_index("expert")
    tokens, width = tok_ref.shape
    slices = zb.shape[0]
    hidden = slices * LANES
    layers = nodes // 4
    ahead = layers // 2
    behind = layers - 1 - ahead
    model_scale = 1.0 / math.sqrt(width)
    hidden_scale = 1.0 / math.sqrt(hidden)
    core = lax.rem(node, 2)
    side = lax.rem(node // 2, 2)
    layer = node // 4
    following = lax.rem(node + 1, nodes)
    previous = lax.rem(node + nodes - 1, nodes)
    other_core = node + 1 - 2 * core
    other_side = node + 2 - 4 * side
    above = lax.rem(node + 4, nodes)
    below = lax.rem(node + nodes - 4, nodes)
    half = experts // 2
    my_hi, my_lo = me // half, lax.rem(me, half)

    def peer(k):
        return lax.rem(my_hi + k // half, 2) * half + lax.rem(my_lo + k % half, half)

    def load(s, part):
        return pltpu.make_async_copy(
            num_ref.at[0, 0, :, pl.ds(part * hidden + s * LANES, LANES)],
            zb.at[s, :, pl.ds(part * LANES, LANES)],
            load_sem.at[s, part],
        )

    for s in range(slices):
        for part in range(3):
            load(s, part).start()

    barrier = pltpu.get_barrier_semaphore()
    for other in (following, previous, other_core, other_side, above, below):
        pl.semaphore_signal(barrier, inc=1, device_id=(other, me), device_id_type=MESH)
    for k in range(1, experts):
        pl.semaphore_signal(barrier, inc=1, device_id=(node, peer(k)), device_id_type=MESH)

    expert_of = lax.broadcasted_iota(jnp.int32, (experts, tokens), 0)
    first = route_ref[0:1, :] == expert_of
    second = route_ref[1:2, :] == expert_of
    gate = jnp.where(first, gate_ref[0:1, :], 0.0) + jnp.where(second, gate_ref[1:2, :], 0.0)
    named = jnp.where(first | second, 1.0, 0.0)
    upto = (
        lax.broadcasted_iota(jnp.int32, (tokens, tokens), 0)
        <= lax.broadcasted_iota(jnp.int32, (tokens, tokens), 1)
    )
    count = jnp.dot(
        named.astype(BF16), jnp.where(upto, 1.0, 0.0).astype(BF16), preferred_element_type=F32
    )
    rank = jnp.where(named > 0.0, count - 1.0, -1.0)
    slot = lax.broadcasted_iota(jnp.int32, (slots, tokens), 0).astype(F32)
    placing, slot_gate = [], []
    for e in range(experts):
        place = slot == rank[e : e + 1, :]
        placing.append(jnp.where(place, 1.0, 0.0))
        slot_gate.append(jnp.sum(jnp.where(place, gate[e : e + 1, :], 0.0), axis=1, keepdims=True))
    placing = jnp.concatenate(placing, axis=0).astype(BF16)
    slot_gate = jnp.concatenate(slot_gate, axis=0)
    x_all = jnp.dot(placing, tok_ref[...], preferred_element_type=F32).astype(BF16)
    x_out[...] = x_all.reshape(experts, slots, width)
    g_all = (jnp.dot(placing, cot_ref[...], preferred_element_type=F32) * slot_gate).astype(BF16)
    g_out[...] = g_all.reshape(experts, slots, width)

    pl.semaphore_wait(barrier, 6 + experts - 1)

    def exchange(k, source, target, send, recv):
        return pltpu.make_async_remote_copy(
            src_ref=source.at[peer(k)],
            dst_ref=target.at[me],
            send_sem=send.at[k],
            recv_sem=recv.at[k],
            device_id=(node, peer(k)),
            device_id_type=MESH,
        )

    for k in range(1, experts):
        exchange(k, x_out, x_in, x_send, x_recv).start()
    for k in range(1, experts):
        exchange(k, g_out, g_in, g_send, g_recv).start()
    x_in[me] = x_out[me]
    g_in[me] = g_out[me]

    def weight(i):
        return jnp.full((1, 3 * LANES), pw_ref[lax.rem(i + 2 * nodes, nodes)], F32)

    def after_one(i):
        return (weight(i) + weight(i - 1)) / 2.0

    def after_two(i):
        return (after_one(i) + after_one(i - 2)) / 2.0

    inverse_first = 1.0 / weight(node)
    inverse_second = 1.0 / after_one(node)
    factor = (0.5 / after_two(node) + 0.5 / after_two(node + 2)) / nodes

    rows = experts * slots

    for k in range(1, experts):
        exchange(k, x_out, x_in, x_send, x_recv).wait_recv()
    x_tr[...] = x_in[...].reshape(rows, width).T
    for k in range(1, experts):
        exchange(k, g_out, g_in, g_send, g_recv).wait_recv()
    g_tr[...] = g_in[...].reshape(rows, width).T

    def hidden_parts():
        pre = (
            jnp.dot(
                x_in[...].reshape(rows, width),
                par[:, : 2 * LANES],
                preferred_element_type=F32,
            )
            * model_scale
        )
        grad_act = (
            jnp.dot(
                g_in[...].reshape(rows, width),
                par[:, 2 * LANES :],
                preferred_element_type=F32,
            )
            * hidden_scale
        )
        pre_gate, pre_up = pre[:, :LANES], pre[:, LANES:]
        sig = 1.0 / (1.0 + jnp.exp(-pre_gate))
        act[:, 2 * LANES :] = (pre_gate * sig * pre_up).astype(BF16)
        act[:, :LANES] = (
            grad_act * pre_up * sig * (1.0 + pre_gate * (1.0 - sig))
        ).astype(BF16)
        act[:, LANES : 2 * LANES] = (grad_act * pre_gate * sig).astype(BF16)

    def gradient(rs):
        of_x = jnp.dot(x_tr[rs, :], act[:, : 2 * LANES], preferred_element_type=F32)
        of_g = jnp.dot(g_tr[rs, :], act[:, 2 * LANES :], preferred_element_type=F32)
        return jnp.concatenate([of_x * model_scale, of_g * hidden_scale], axis=1)

    blocks = width // ROW_STEP

    def pass_on(s):
        return pltpu.make_async_remote_copy(
            src_ref=pushed.at[s],
            dst_ref=arrived.at[s],
            send_sem=b_send.at[s],
            recv_sem=b_recv.at[s],
            device_id=(following, me),
            device_id_type=MESH,
        )

    def round_one(s, carry):
        for part in range(3):
            load(s, part).wait()

        def to_params(b, c):
            rs = pl.ds(pl.multiple_of(b * ROW_STEP, ROW_STEP), ROW_STEP)
            par[rs, :] = (zb[s, rs, :].astype(F32) * inverse_first).astype(BF16)
            return c

        lax.fori_loop(0, blocks, to_params, 0)
        hidden_parts()

        def update(b, c):
            rs = pl.ds(pl.multiple_of(b * ROW_STEP, ROW_STEP), ROW_STEP)
            pushed[s, rs, :] = (zb[s, rs, :].astype(F32) - gradient(rs)).astype(BF16)
            return c

        lax.fori_loop(0, blocks, update, 0)
        pass_on(s).start()
        return carry

    lax.fori_loop(0, slices, round_one, 0)

    def share_copy(s):
        return pltpu.make_async_remote_copy(
            src_ref=share.at[s, 1 - core],
            dst_ref=share_in.at[s],
            send_sem=c_send.at[s],
            recv_sem=c_recv.at[s],
            device_id=(other_core, me),
            device_id_type=MESH,
        )

    def ring_copy(s, step):
        return pltpu.make_async_remote_copy(
            src_ref=ring_out.at[s, step],
            dst_ref=ring_in.at[s, step],
            send_sem=r_send.at[s, step],
            recv_sem=r_recv.at[s, step],
            device_id=(above if step < ahead else below, me),
            device_id_type=MESH,
        )

    def side_copy(s):
        return pltpu.make_async_remote_copy(
            src_ref=side_out.at[s],
            dst_ref=side_in.at[s],
            send_sem=s_send.at[s],
            recv_sem=s_recv.at[s],
            device_id=(other_side, me),
            device_id_type=MESH,
        )

    def own_sum(s, d):
        at = pl.ds(2 * d, 2)
        return share[s, core, at].astype(F32) + share_in[s, at].astype(F32)

    def ring_step(s, t):
        if t < ahead:
            total = own_sum(s, lax.rem(layer + ahead - t, layers))
            if t > 0:
                ring_copy(s, t - 1).wait_recv()
                total = total + ring_in[s, t - 1].astype(F32)
            ring_out[s, t] = total.astype(BF16)
            ring_copy(s, t).start()
        if t < behind:
            total = own_sum(s, lax.rem(layer + layers - behind + t, layers))
            if t > 0:
                ring_copy(s, ahead + t - 1).wait_recv()
                total = total + ring_in[s, ahead + t - 1].astype(F32)
            ring_out[s, ahead + t] = total.astype(BF16)
            ring_copy(s, ahead + t).start()

    def begin_ring(s):
        share_copy(s).wait_recv()
        ring_step(s, 0)

    def end_ring(s):
        total = own_sum(s, layer)
        ring_copy(s, ahead + behind - 1).wait_recv()
        total = total + ring_in[s, ahead + behind - 1].astype(F32)
        ring_copy(s, ahead - 1).wait_recv()
        total = total + ring_in[s, ahead - 1].astype(F32)
        kept[s] = total
        side_out[s] = kept[s, 1 - side].astype(BF16)
        side_copy(s).start()

    def finish(s):
        side_copy(s).wait_recv()
        total = kept[s, side] + side_in[s].astype(F32)
        for part in range(3):
            at = pl.ds(pl.multiple_of(part * hidden + s * LANES, LANES), LANES)
            out_ref[0, :, at] = total[:, part * LANES : (part + 1) * LANES]

    def round_two(s, carry):
        pass_on(s).wait_recv()

        def to_params(b, c):
            rs = pl.ds(pl.multiple_of(b * ROW_STEP, ROW_STEP), ROW_STEP)
            mixed = (
                (pushed[s, rs, :].astype(F32) + arrived[s, rs, :].astype(F32)) / 2.0
            ).astype(BF16)
            zb[s, rs, :] = mixed
            par[rs, :] = (mixed.astype(F32) * inverse_second).astype(BF16)
            return c

        lax.fori_loop(0, blocks, to_params, 0)
        hidden_parts()
        groups = ROW_STEP // (2 * out_ref.shape[1])

        def update(b, c):
            rs = pl.ds(pl.multiple_of(b * ROW_STEP, ROW_STEP), ROW_STEP)
            new = (zb[s, rs, :].astype(F32) - gradient(rs)).astype(BF16)
            term = (new.astype(F32) * factor).astype(BF16)
            term = term.reshape(groups, 2, out_ref.shape[1], 3 * LANES)
            at = pl.ds(b * groups, groups)
            share[s, 0, at] = term[:, 0]
            share[s, 1, at] = term[:, 1]
            return c

        lax.fori_loop(0, blocks, update, 0)
        share_copy(s).start()
        pl.when(s > 0)(lambda: ring_step(s - 1, 3))
        begin_ring(s)
        pl.when(s > 0)(lambda: end_ring(s - 1))
        ring_step(s, 1)
        pl.when(s > 0)(lambda: finish(s - 1))
        ring_step(s, 2)
        return carry

    lax.fori_loop(0, slices, round_two, 0)
    ring_step(slices - 1, 3)
    end_ring(slices - 1)
    finish(slices - 1)

    for k in range(1, experts):
        exchange(k, x_out, x_in, x_send, x_recv).wait_send()
        exchange(k, g_out, g_in, g_send, g_recv).wait_send()

    def drain(s, carry):
        pass_on(s).wait_send()
        share_copy(s).wait_send()
        for t in range(ahead + behind):
            ring_copy(s, t).wait_send()
        side_copy(s).wait_send()
        return carry

    lax.fori_loop(0, slices, drain, 0)


def local(nodes, experts, numerators, push_weights, tokens, cotangent, routing, gates):
    width = numerators.shape[2]
    hidden = numerators.shape[3] // 3
    rows = tokens.shape[1]
    choose = routing.shape[2]
    capacity = min(rows, rows * choose * 5 // (4 * experts) + 1)
    slots = -(-capacity // 16) * 16
    slices = hidden // LANES
    out_rows = width // nodes
    all_rows = experts * slots
    pieces = nodes // 2
    steps = nodes // 4 - 1
    dma = pltpu.SemaphoreType.DMA
    vmem = pl.BlockSpec(memory_space=pltpu.VMEM)
    return pl.pallas_call(
        functools.partial(kernel, nodes, experts, slots),
        out_shape=jax.ShapeDtypeStruct((1, out_rows, 3 * hidden), F32),
        in_specs=[
            pl.BlockSpec(memory_space=pltpu.SMEM),
            vmem,
            vmem,
            vmem,
            vmem,
            pl.BlockSpec(memory_space=pl.ANY),
        ],
        out_specs=vmem,
        scratch_shapes=[
            pltpu.VMEM((experts, slots, width), BF16),
            pltpu.VMEM((experts, slots, width), BF16),
            pltpu.VMEM((experts, slots, width), BF16),
            pltpu.VMEM((experts, slots, width), BF16),
            pltpu.VMEM((width, all_rows), BF16),
            pltpu.VMEM((width, all_rows), BF16),
            pltpu.VMEM((slices, width, 3 * LANES), BF16),
            pltpu.VMEM((width, 3 * LANES), BF16),
            pltpu.VMEM((all_rows, 3 * LANES), BF16),
            pltpu.VMEM((slices, width, 3 * LANES), BF16),
            pltpu.VMEM((slices, width, 3 * LANES), BF16),
            pltpu.VMEM((slices, 2, pieces, out_rows, 3 * LANES), BF16),
            pltpu.VMEM((slices, pieces, out_rows, 3 * LANES), BF16),
            pltpu.VMEM((slices, steps, 2, out_rows, 3 * LANES), BF16),
            pltpu.VMEM((slices, steps, 2, out_rows, 3 * LANES), BF16),
            pltpu.VMEM((slices, out_rows, 3 * LANES), BF16),
            pltpu.VMEM((slices, out_rows, 3 * LANES), BF16),
            pltpu.VMEM((slices, 2, out_rows, 3 * LANES), F32),
            dma((slices, 3)),
            dma((experts,)),
            dma((experts,)),
            dma((experts,)),
            dma((experts,)),
            dma((slices,)),
            dma((slices,)),
            dma((slices,)),
            dma((slices,)),
            dma((slices, steps)),
            dma((slices, steps)),
            dma((slices,)),
            dma((slices,)),
        ],
        compiler_params=pltpu.CompilerParams(
            collective_id=0, has_side_effects=True, vmem_limit_bytes=60 * 1024 * 1024
        ),
    )(push_weights, routing[0].T, gates[0].T, tokens[0], cotangent[0], numerators)


def solution(mesh):
    placed = (
        P("node", "expert", None, None),
        P(),
        P("node", "expert", None),
        P("node", "expert", None),
        P("node", "expert", None),
        P("node", "expert", None),
    )
    return jax.shard_map(
        functools.partial(local, mesh.shape["node"], mesh.shape["expert"]),
        mesh=mesh,
        in_specs=placed,
        out_specs=P("expert", "node", None),
        check_vma=False,
    )
```

time: 251 us -> 152 us (0.61)
  Pallas kernels: 0 us -> 147 us
  blocking collectives: 120 us -> 0 us
  waiting for transfers between devices: 64.6 us -> 0 us
  other arithmetic: 20.4 us -> 0 us
  local copies, waits for them, and re-layouts: 20 us -> 1.69 us
  matrix products: 15.9 us -> 0 us
  starting transfers between devices: 9.22 us -> 0 us
    pallas_call x0 -> x1, Pallas kernels: none -> 147 us  [local(): pl.pallas_call(functools.partial(kernel, nodes, experts, slots), out_shap...]
    all_to_all x1 -> x0, blocking collectives: 120 us -> none  [sent_and_summed(): lax.all_to_all(parts, axis, split_axis=0, concat_axis=0, tiled=True)]
    ppermute x1 -> x0, waiting for transfers between devices: 48.9 us -> none  [passed_along(): lax.ppermute(shard, axis, [(i, (i + by) % count) for i in range(count)])]
    dot_general x13 -> x0, matrix products: 15.9 us -> none  [the longest x2 3.27 us: expert_grads(): jnp.einsum('wqv,qvy->wqy', buffer_inputs, gate_weight_matrix, preferred_e...]
    all_to_all x1 -> x0, waiting for transfers between devices: 15.7 us -> none  [side_by_side(): lax.all_to_all(both, axis, split_axis=split_dim, concat_axis=concat_dim,...]
    squeeze x2 -> x0, other arithmetic: 8.42 us -> none  [local(): gradients = expert_grads(params[0], recv_inputs, recv_grads)]
    all_to_all x1 -> x0, starting transfers between devices: 7.61 us -> none  [side_by_side(): lax.all_to_all(both, axis, split_axis=split_dim, concat_axis=concat_dim,...]
    convert_element_type x1 -> x0, local copies, waits for them, and re-layouts: 6.71 us -> none  [local(): return sent_and_summed(summand[0].astype(jnp.bfloat16), 'node', 1)]
  transfers between devices with their start and end apart: 2 -> 0, of which waited for: 2 -> 0; matrix products, arithmetic and copies ran while one was open for 6% -> 0% of each run, Pallas kernels for 0% -> 0%
where the time goes in v1:
time: 152 us; the launch traced here: 149 us
  Pallas kernels  147 us (97%)
  local copies, waits for them, and re-layouts  1.69 us (1%)
    pallas_call x1, Pallas kernels, local(): pl.pallas_call(functools.partial(kernel, nodes, experts, slots), out_shap...  147 us

profile of v1, /device:TPU:1, one launch (start us, length us, event | category | flops | bytes accessed | tf_op | source)
XLA Modules:
  0.0 149.1 jit_solution(17124545350542006118)
XLA Ops:
  0.0 147.4 %shard_map.64 = f32[1,48,1536]{2,1,0:T(8,128)} custom-call(f32[32]{0:T(128)} %pw_ref.1, s32[2,128]{1,0:T(2,128)} %bitcast.10, f32[2,128]{1,0:T(2,128)} %bitcast.11, bf16[128,1536]{1,0:T(8,128)(2,1)} %bitcast.8, bf16[128,1536]{1,0:T(8,128)(2,1)} %bitcast.9, bf16[1,1,1536,1536]{3,2,1,0:T(8,128)(2,1)} %num_ref.1), custom_call_target="tpu_custom_call" | custom-call | tf_op jit(solution)/shard_map/pallas_call | solution.py:376
  147.4 1.7 %copy.8 = f32[1,48,1536]{2,1,0:T(8,128)} copy(f32[1,48,1536]{2,1,0:T(8,128)} %shard_map.64) | data formatting | bytes 589824

commit v2 on v1

--- a/solution.py
+++ b/solution.py
@@ -65,7 +65,7 @@
     hidden = slices * LANES
     layers = nodes // 4
     ahead = layers // 2
-    behind = layers - 1 - ahead
+    steps = layers - 1
     model_scale = 1.0 / math.sqrt(width)
     hidden_scale = 1.0 / math.sqrt(hidden)
     core = lax.rem(node, 2)
@@ -199,12 +199,13 @@
 
     blocks = width // ROW_STEP
 
-    def pass_on(s):
+    def pass_on(s, b):
+        rs = pl.ds(pl.multiple_of(b * ROW_STEP, ROW_STEP), ROW_STEP)
         return pltpu.make_async_remote_copy(
-            src_ref=pushed.at[s],
-            dst_ref=arrived.at[s],
-            send_sem=b_send.at[s],
-            recv_sem=b_recv.at[s],
+            src_ref=pushed.at[s, rs],
+            dst_ref=arrived.at[s, rs],
+            send_sem=b_send.at[s, b],
+            recv_sem=b_recv.at[s, b],
             device_id=(following, me),
             device_id_type=MESH,
         )
@@ -224,10 +225,11 @@
         def update(b, c):
             rs = pl.ds(pl.multiple_of(b * ROW_STEP, ROW_STEP), ROW_STEP)
             pushed[s, rs, :] = (zb[s, rs, :].astype(F32) - gradient(rs)).astype(BF16)
+            pl.when(b > 0)(lambda: pass_on(s, b - 1).start())
             return c
 
         lax.fori_loop(0, blocks, update, 0)
-        pass_on(s).start()
+        pass_on(s, blocks - 1).start()
         return carry
 
     lax.fori_loop(0, slices, round_one, 0)
@@ -242,13 +244,13 @@
             device_id_type=MESH,
         )
 
-    def ring_copy(s, step):
+    def ring_copy(s, step, q, up):
         return pltpu.make_async_remote_copy(
-            src_ref=ring_out.at[s, step],
-            dst_ref=ring_in.at[s, step],
-            send_sem=r_send.at[s, step],
-            recv_sem=r_recv.at[s, step],
-            device_id=(above if step < ahead else below, me),
+            src_ref=ring_out.at[s, step, q],
+            dst_ref=ring_in.at[s, step, q],
+            send_sem=r_send.at[s, step, q],
+            recv_sem=r_recv.at[s, step, q],
+            device_id=(above if up else below, me),
             device_id_type=MESH,
         )
 
@@ -262,39 +264,50 @@
             device_id_type=MESH,
         )
 
-    def own_sum(s, d):
-        at = pl.ds(2 * d, 2)
-        return share[s, core, at].astype(F32) + share_in[s, at].astype(F32)
+    def own_sum(s, d, q):
+        return share[s, core, 2 * d + q].astype(F32) + share_in[s, 2 * d + q].astype(F32)
+
+    def hops_up(s):
+        return jnp.where((side == 1) & (s < slices - 1), 0, ahead)
+
+    halves = (1 - side, side)
 
     def ring_step(s, t):
+        hops = hops_up(s)
+
+        def move(step, d, up):
+            for q in halves:
+                total = own_sum(s, d, q)
+                if t > 0:
+                    ring_copy(s, step - 1, q, up).wait_recv()
+                    total = total + ring_in[s, step - 1, q].astype(F32)
+                ring_out[s, step, q] = total.astype(BF16)
+                ring_copy(s, step, q, up).start()
+
         if t < ahead:
-            total = own_sum(s, lax.rem(layer + ahead - t, layers))
-            if t > 0:
-                ring_copy(s, t - 1).wait_recv()
-                total = total + ring_in[s, t - 1].astype(F32)
-            ring_out[s, t] = total.astype(BF16)
-            ring_copy(s, t).start()
-        if t < behind:
-            total = own_sum(s, lax.rem(layer + layers - behind + t, layers))
-            if t > 0:
-                ring_copy(s, ahead + t - 1).wait_recv()
-                total = total + ring_in[s, ahead + t - 1].astype(F32)
-            ring_out[s, ahead + t] = total.astype(BF16)
-            ring_copy(s, ahead + t).start()
+            pl.when(t < hops)(lambda: move(t, lax.rem(layer + hops - t, layers), True))
+        pl.when(t < steps - hops)(
+            lambda: move(hops + t, lax.rem(layer + layers - steps + hops + t, layers), False)
+        )
 
     def begin_ring(s):
         share_copy(s).wait_recv()
         ring_step(s, 0)
 
     def end_ring(s):
-        total = own_sum(s, layer)
-        ring_copy(s, ahead + behind - 1).wait_recv()
-        total = total + ring_in[s, ahead + behind - 1].astype(F32)
-        ring_copy(s, ahead - 1).wait_recv()
-        total = total + ring_in[s, ahead - 1].astype(F32)
-        kept[s] = total
-        side_out[s] = kept[s, 1 - side].astype(BF16)
-        side_copy(s).start()
+        hops = hops_up(s)
+        for q in halves:
+            ring_copy(s, steps - 1, q, False).wait_recv()
+            kept[s, q] = own_sum(s, layer, q) + ring_in[s, steps - 1, q].astype(F32)
+
+            def add_upward():
+                ring_copy(s, ahead - 1, q, True).wait_recv()
+                kept[s, q] += ring_in[s, ahead - 1, q].astype(F32)
+
+            pl.when(hops > 0)(add_upward)
+            if q is halves[0]:
+                side_out[s] = kept[s, q].astype(BF16)
+                side_copy(s).start()
 
     def finish(s):
         side_copy(s).wait_recv()
@@ -304,10 +317,9 @@
             out_ref[0, :, at] = total[:, part * LANES : (part + 1) * LANES]
 
     def round_two(s, carry):
-        pass_on(s).wait_recv()
-
         def to_params(b, c):
             rs = pl.ds(pl.multiple_of(b * ROW_STEP, ROW_STEP), ROW_STEP)
+            pass_on(s, b).wait_recv()
             mixed = (
                 (pushed[s, rs, :].astype(F32) + arrived[s, rs, :].astype(F32)) / 2.0
             ).astype(BF16)
@@ -331,28 +343,37 @@
 
         lax.fori_loop(0, blocks, update, 0)
         share_copy(s).start()
-        pl.when(s > 0)(lambda: ring_step(s - 1, 3))
+        pl.when(s >= 1)(lambda: ring_step(s - 1, 2))
+        pl.when(s >= 2)(lambda: ring_step(s - 2, 5))
         begin_ring(s)
-        pl.when(s > 0)(lambda: end_ring(s - 1))
+        pl.when(s >= 1)(lambda: ring_step(s - 1, 3))
+        pl.when(s >= 2)(lambda: ring_step(s - 2, 6))
         ring_step(s, 1)
-        pl.when(s > 0)(lambda: finish(s - 1))
-        ring_step(s, 2)
+        pl.when(s >= 1)(lambda: ring_step(s - 1, 4))
+        pl.when(s >= 2)(lambda: end_ring(s - 2))
         return carry
 
     lax.fori_loop(0, slices, round_two, 0)
+    ring_step(slices - 1, 2)
+    ring_step(slices - 2, 5)
     ring_step(slices - 1, 3)
+    ring_step(slices - 2, 6)
     end_ring(slices - 1)
-    finish(slices - 1)
+    end_ring(slices - 2)
+    for s in range(slices):
+        finish(s)
 
     for k in range(1, experts):
         exchange(k, x_out, x_in, x_send, x_recv).wait_send()
         exchange(k, g_out, g_in, g_send, g_recv).wait_send()
 
     def drain(s, carry):
-        pass_on(s).wait_send()
+        for b in range(blocks):
+            pass_on(s, b).wait_send()
         share_copy(s).wait_send()
-        for t in range(ahead + behind):
-            ring_copy(s, t).wait_send()
+        for t in range(steps):
+            for q in range(2):
+                ring_copy(s, t, q, True).wait_send()
         side_copy(s).wait_send()
         return carry
 
@@ -409,12 +430,12 @@
             dma((experts,)),
             dma((experts,)),
             dma((experts,)),
+            dma((slices, width // ROW_STEP)),
+            dma((slices, width // ROW_STEP)),
             dma((slices,)),
             dma((slices,)),
-            dma((slices,)),
-            dma((slices,)),
-            dma((slices, steps)),
-            dma((slices, steps)),
+            dma((slices, steps, 2)),
+            dma((slices, steps, 2)),
             dma((slices,)),
             dma((slices,)),
         ],

time: 152 us -> 120 us (0.79)
  Pallas kernels: 147 us -> 116 us
    pallas_call x1, Pallas kernels: 147 us -> 116 us  [local(): pl.pallas_call(functools.partial(kernel, nodes, experts, slots), out_shap...]
where the time goes in v2:
time: 120 us; the launch traced here: 118 us
  Pallas kernels  116 us (97%)
  local copies, waits for them, and re-layouts  1.69 us (1%)
    pallas_call x1, Pallas kernels, local(): pl.pallas_call(functools.partial(kernel, nodes, experts, slots), out_shap...  116 us

profile of v2, /device:TPU:1, one launch (start us, length us, event | category | flops | bytes accessed | tf_op | source)
XLA Modules:
  0.0 117.8 jit_solution(3524646666223226988)
XLA Ops:
  0.0 116.1 %shard_map.64 = f32[1,48,1536]{2,1,0:T(8,128)} custom-call(f32[32]{0:T(128)} %pw_ref.1, s32[2,128]{1,0:T(2,128)} %bitcast.10, f32[2,128]{1,0:T(2,128)} %bitcast.11, bf16[128,1536]{1,0:T(8,128)(2,1)} %bitcast.8, bf16[128,1536]{1,0:T(8,128)(2,1)} %bitcast.9, bf16[1,1,1536,1536]{3,2,1,0:T(8,128)(2,1)} %num_ref.1), custom_call_target="tpu_custom_call" | custom-call | tf_op jit(solution)/shard_map/pallas_call | solution.py:397
  116.1 1.7 %copy.8 = f32[1,48,1536]{2,1,0:T(8,128)} copy(f32[1,48,1536]{2,1,0:T(8,128)} %shard_map.64) | data formatting | bytes 589824
